TPU v7x, 128 devices: a whole 4x4x4 slice. The times are simulated.
128 devices in a mesh: batch: 32 (over z, x, core), cols: 4 (over y).
Axes of the slice: x: 4, y: 4, z: 4, core: 2. Of those that a mesh axis runs over, the one named last changes fastest.
Arguments:
- partial_query: float32 [32, 1024, 1024], P('batch', None, 'cols'), may hold values from -1.25 to 1.25
- partial_key: float32 [32, 1024, 1024], P('batch', None, 'cols'), may hold values from -1.25 to 1.25
- partial_value: float32 [32, 1024, 1024], P('batch', None, 'cols'), may hold values from -1.25 to 1.25
- partial_mixed: float32 [32, 1024, 1024], P('batch', 'cols'), may hold values from -1.25 to 1.25
- partial_norm: float32 [32, 1024], P('batch'), may hold values from -12 to 12
- partial_bias: float32 [32, 1024], P('batch'), may hold values from -12 to 12
- master_query: float32 [1024, 1024], P('batch', 'cols'), may hold values from -0.1875 to 0.1875
- master_key: float32 [1024, 1024], P('batch', 'cols'), may hold values from -0.1875 to 0.1875
- master_value: float32 [1024, 1024], P('batch', 'cols'), may hold values from -0.1875 to 0.1875
- master_mixed: float32 [1024, 1024], P('cols', 'batch'), may hold values from -0.1875 to 0.1875
- master_norm: float32 [1024], P('batch'), may hold values from 0.25 to 1.75
- master_bias: float32 [1024], P('batch'), may hold values from -3 to 3
Outputs:
- compute_query: bfloat16 [1024, 1024], P(None, 'cols')
- compute_key: bfloat16 [1024, 1024], P(None, 'cols')
- compute_value: bfloat16 [1024, 1024], P(None, 'cols')
- compute_mixed: bfloat16 [1024, 1024], P('cols')
- compute_norm: bfloat16 [1024], replicated
- compute_bias: bfloat16 [1024], replicated
- stepped_query: float32 [1024, 1024], P('batch', 'cols')
- stepped_key: float32 [1024, 1024], P('batch', 'cols')
- stepped_value: float32 [1024, 1024], P('batch', 'cols')
- stepped_mixed: float32 [1024, 1024], P('cols', 'batch')
- stepped_norm: float32 [1024], P('batch')
- stepped_bias: float32 [1024], P('batch')
All inputs are finite; a program needn't handle non-finite values.
Results may differ from a plain program's by a relative error of at most 0.001.
Values may be sent and summed in bfloat16 or wider, within the bound.
A program may use at most 64 MiB of HBM per device.

v0:
```python
import jax
import jax.numpy as jnp
from jax import lax
from jax.sharding import Mesh
from jax.sharding import PartitionSpec as P

BATCH = ("batch_0", "batch_1", "batch_2")
learn_rate = 0.4


def in_blocks(x, dim, count):
    shape = x.shape
    tiles = x.reshape(*shape[:dim], count, shape[dim] // count, *shape[dim + 1 :])
    return jnp.moveaxis(tiles, dim, 0)


def sent_and_summed(x, axis, dim):
    count = lax.axis_size(axis)
    tiles = lax.all_to_all(in_blocks(x, dim, count), axis, 0, 0, tiled=True)
    return jnp.sum(tiles, axis=0)


def sum_by_axis(x, axes, dim):
    far, near = axes
    own = sent_and_summed(in_blocks(x, dim, lax.axis_size(far)), near, dim + 1)
    return jnp.sum(lax.all_to_all(own, far, 0, 0, tiled=True), axis=0)


def side_by_side(arrays, axis, dim, along):
    ends, at = ([], 0)
    for a in arrays[:-1]:
        at += a.shape[along]
        ends.append(at)
    both = jnp.concatenate(arrays, axis=along)
    return tuple(jnp.split(sum_by_axis(both, axis, dim), ends, axis=along))


def gather_turned(arrays, axis, dims):
    turned = [jnp.moveaxis(a, dim, 0) for a, dim in zip(arrays, dims)]
    both = jnp.concatenate([t.reshape(len(t), -1) for t in turned], axis=1)
    whole, at, done = (lax.all_gather(both, axis, axis=0, tiled=True), 0, [])
    for t, dim in zip(turned, dims):
        share = whole[:, at : at + t[0].size].reshape(-1, *t.shape[1:])
        done.append(jnp.moveaxis(share, 0, dim))
        at += t[0].size
    return tuple(done)


def per_device(
    partial_query,
    partial_key,
    partial_value,
    partial_mixed,
    partial_norm,
    partial_bias,
    master_query,
    master_key,
    master_value,
    master_mixed,
    master_norm,
    master_bias,
):
    mean_query, mean_key, mean_value, mean_mixed, mean_norm, mean_bias = (
        *side_by_side(
            (partial_query[0], partial_key[0], partial_value[0]),
            (("batch_0", "batch_1"), "batch_2"),
            0,
            1,
        ),
        sum_by_axis(partial_mixed[0], (("batch_0", "batch_1"), "batch_2"), 1),
        sum_by_axis(partial_norm[0], (("batch_0", "batch_1"), "batch_2"), 0),
        sum_by_axis(partial_bias[0], (("batch_0", "batch_1"), "batch_2"), 0),
    )
    mean_rate = lax.axis_size(BATCH) ** (-0.5)
    mean_query = mean_query * mean_rate
    mean_key = mean_key * mean_rate
    mean_value = mean_value * mean_rate
    mean_mixed = mean_mixed * mean_rate
    mean_norm = mean_norm * mean_rate
    mean_bias = mean_bias * mean_rate
    stepped_query = master_query - learn_rate * mean_query
    stepped_key = master_key - learn_rate * mean_key
    stepped_value = master_value - learn_rate * mean_value
    stepped_mixed = master_mixed - learn_rate * mean_mixed
    stepped_norm = master_norm - learn_rate * mean_norm
    stepped_bias = master_bias - learn_rate * mean_bias
    compute_query, compute_key, compute_value, compute_mixed, compute_norm, compute_bias = (
        gather_turned(
            (
                stepped_query.astype(jnp.bfloat16),
                stepped_key.astype(jnp.bfloat16),
                stepped_value.astype(jnp.bfloat16),
                stepped_mixed.astype(jnp.bfloat16),
                stepped_norm.astype(jnp.bfloat16),
                stepped_bias.astype(jnp.bfloat16),
            ),
            BATCH,
            (0, 0, 0, 1, 0, 0),
        )
    )
    return (
        compute_query,
        compute_key,
        compute_value,
        compute_mixed,
        compute_norm,
        compute_bias,
        stepped_query,
        stepped_key,
        stepped_value,
        stepped_mixed,
        stepped_norm,
        stepped_bias,
    )


def solution(mesh):
    split = Mesh(
        mesh.devices.reshape(4, 4, 2, mesh.shape["cols"]), ("batch_0", "batch_1", "batch_2", "cols")
    )
    in_specs = (
        P(BATCH, None, "cols"),
        P(BATCH, None, "cols"),
        P(BATCH, None, "cols"),
        P(BATCH, "cols", None),
        P(BATCH, None),
        P(BATCH, None),
        P(BATCH, "cols"),
        P(BATCH, "cols"),
        P(BATCH, "cols"),
        P("cols", BATCH),
        P(BATCH),
        P(BATCH),
    )
    out_specs = (
        P(None, "cols"),
        P(None, "cols"),
        P(None, "cols"),
        P("cols", None),
        P(),
        P(),
        P(BATCH, "cols"),
        P(BATCH, "cols"),
        P(BATCH, "cols"),
        P("cols", BATCH),
        P(BATCH),
        P(BATCH),
    )
    return jax.shard_map(
        per_device, mesh=split, in_specs=in_specs, out_specs=out_specs, check_vma=False
    )
```

profile of v0, /device:TPU:1, one launch (start us, length us, event | category | flops | bytes accessed | tf_op | source)
XLA Modules:
  0.0 161.0 jit_solution(4723989277255362857)
XLA Ops:
  7.2 0.5 broadcast.18
  7.7 1.3 reduce.12
  9.0 0.1 reshape_reshape_squeeze.6
  9.1 0.7 reshape.72
  9.8 4.6 %all-to-all-start.4 = ((f32[2,1,512]{2,1,0:T(1,128)}), f32[2,1,512]{2,1,0:T(1,128)S(1)}, u32[]{:S(2)}, u32[]{:S(2)}) async-start(f32[2,1,512]{2,1,0:T(1,128)} %reshape.72), calls=%async_computation.4 | async-start | bytes 8192 | tf_op jit(solution)/shard_map/all_to_all | solution.py:19
  14.4 2.2 %maximum_bitcast_fusion = f32[2,16,32,768]{3,2,0,1:T(8,128)S(1)} fusion(f32[16,2,32,256]{3,2,1,0:T(8,128)} %bitcast.25, f32[16,2,32,256]{3,2,1,0:T(8,128)} %bitcast.26, f32[16,2,32,256]{3,2,1,0:T(8,128)} %bitcast.27), kind=kLoop, calls=%fused_computation | loop fusion | flops 1572864 | bytes 6291456 | tf_op jit(solution)/shard_map/transpose | solution.py:14
  16.6 2.0 %copy.46 = f32[2,16,32,768]{3,2,1,0:T(8,128)} copy(f32[2,16,32,768]{3,2,0,1:T(8,128)S(1)} %maximum_bitcast_fusion) | data formatting | bytes 6291456 | tf_op jit(solution)/shard_map/transpose | solution.py:14
  18.6 0.0 copy-start.4
  18.6 0.0 all-to-all-done.4
  18.6 4.1 %all-to-all-start = ((f32[2,16,32,768]{3,2,1,0:T(8,128)}), f32[2,16,32,768]{3,2,1,0:T(8,128)S(1)}, u32[]{:S(2)}, u32[]{:S(2)}) async-start(f32[2,16,32,768]{3,2,1,0:T(8,128)} %copy.46), calls=%async_computation | async-start | bytes 6291456 | tf_op jit(solution)/shard_map/all_to_all | solution.py:19
  22.7 0.5 broadcast.20
  23.2 0.7 reduce.14
  23.9 0.1 reshape.73
  24.0 0.0 copy-done.4
  24.0 0.7 reduce.13
  24.6 0.1 reshape_reshape_squeeze.7
  24.7 0.1 reshape.74
  24.8 2.5 %copy.47 = f32[1,256,1024]{1,2,0:T(8,128)} copy(f32[1,256,1024]{2,1,0:T(8,128)} %param.15) | data formatting | bytes 2097152 | tf_op args[3]
  27.3 2.3 %copy.48 = f32[2,16,256,32]{2,3,1,0:T(8,128)} copy(f32[2,16,256,32]{2,3,0,1:T(8,128)} %bitcast.24) | data formatting | bytes 2097152 | tf_op jit(solution)/shard_map/transpose | solution.py:14
  29.7 0.6 reduce_sum.76
  30.3 0.0 all-to-all-done
  30.3 3.4 %all_to_all.48 = f32[2,1,512]{2,1,0:T(1,128)S(1)} all-to-all(f32[2,1,512]{2,1,0:T(1,128)S(1)} %reshape.74), channel_id=1, replica_groups=mesh['batch_0'=4,'batch_1'=4,'batch_2'=2,'cols'=4] {'batch_2'}, dimensions={0} | all-to-all | bytes 8192 | tf_op jit(solution)/shard_map/all_to_all | solution.py:19
  33.6 6.5 %all_to_all.49 = f32[2,16,256,32]{2,3,1,0:T(8,128)} all-to-all(f32[2,16,256,32]{2,3,1,0:T(8,128)} %copy.48), channel_id=1, replica_groups=mesh['batch_0'=4,'batch_1'=4,'batch_2'=2,'cols'=4] {'batch_2'}, dimensions={0} | all-to-all | bytes 2097152 | tf_op jit(solution)/shard_map/all_to_all | solution.py:19
  40.2 7.7 %all-to-all-start.5 = ((f32[16,1,32]{2,1,0:T(1,128)}), f32[16,1,32]{2,1,0:T(1,128)S(1)}, u32[]{:S(2)}, u32[]{:S(2)}) async-start(f32[16,1,32]{2,1,0:T(1,128)} %bitcast.10), calls=%async_computation.5 | async-start | bytes 16384 | tf_op jit(solution)/shard_map/all_to_all | solution.py:26
  47.9 0.7 reduce.15
  48.6 0.1 reshape.75
  48.6 0.6 reduce_sum.78
  49.3 5.0 %all-to-all-done.5 = f32[16,1,32]{2,1,0:T(1,128)S(1)} async-done(((f32[16,1,32]{2,1,0:T(1,128)}), f32[16,1,32]{2,1,0:T(1,128)S(1)}, u32[]{:S(2)}, u32[]{:S(2)}) %all-to-all-start.5) | async-done | bytes 2080 | tf_op jit(solution)/shard_map/all_to_all | solution.py:26
  54.3 3.5 %all-to-all-start.7 = ((f32[16,1,32]{2,1,0:T(1,128)}), f32[16,1,32]{2,1,0:T(1,128)S(1)}, u32[]{:S(2)}, u32[]{:S(2)}) async-start(f32[16,1,32]{2,1,0:T(1,128)} %bitcast.13), calls=%async_computation.7 | async-start | bytes 16384 | tf_op jit(solution)/shard_map/all_to_all | solution.py:26
  57.7 2.1 %reduce_sum.74 = f32[16,256,32]{1,2,0:T(8,128)} reduce(f32[2,16,256,32]{2,3,1,0:T(8,128)} %all_to_all.49, f32[]{:T(128)} %constant.6.clone.1), dimensions={0}, to_apply=%region_2.0 | reduce | flops 131072 | bytes 1572868 | tf_op jit(solution)/shard_map/reduce_sum | solution.py:20
  59.9 4.2 %all-to-all-done.7 = f32[16,1,32]{2,1,0:T(1,128)S(1)} async-done(((f32[16,1,32]{2,1,0:T(1,128)}), f32[16,1,32]{2,1,0:T(1,128)S(1)}, u32[]{:S(2)}, u32[]{:S(2)}) %all-to-all-start.7) | async-done | bytes 2080 | tf_op jit(solution)/shard_map/all_to_all | solution.py:26
  64.0 4.2 %all-to-all-start.3 = ((f32[16,256,32]{1,2,0:T(8,128)}), f32[16,256,32]{1,2,0:T(8,128)}, u32[]{:S(2)}, u32[]{:S(2)}) async-start(f32[16,256,32]{1,2,0:T(8,128)} %reduce_sum.74), calls=%async_computation.3 | async-start | bytes 1048576 | tf_op jit(solution)/shard_map/all_to_all | solution.py:26
  68.3 0.0 copy-start.5
  68.3 0.0 copy-start.6
  68.3 0.0 copy-start
  68.3 1.5 reduce_sum.72
  69.8 0.0 copy-start.1
  69.8 0.0 copy-start.2
  69.8 0.0 copy-start.3
  69.8 7.4 %all-to-all-done.3 = f32[16,256,32]{1,2,0:T(8,128)} async-done(((f32[16,256,32]{1,2,0:T(8,128)}), f32[16,256,32]{1,2,0:T(8,128)}, u32[]{:S(2)}, u32[]{:S(2)}) %all-to-all-start.3) | async-done | bytes 524320 | tf_op jit(solution)/shard_map/all_to_all | solution.py:26
  77.3 3.7 %all-to-all-start.1 = ((f32[16,32,768]{2,1,0:T(8,128)}), f32[16,32,768]{2,1,0:T(8,128)S(1)}, u32[]{:S(2)}, u32[]{:S(2)}) async-start(f32[16,32,768]{2,1,0:T(8,128)} %reduce_sum.72), calls=%async_computation.1 | async-start | bytes 3145728 | tf_op jit(solution)/shard_map/all_to_all | solution.py:26
  81.0 0.0 all-gather.2.cloned.1.call-start
  81.1 0.0 copy-done.5
  81.1 0.5 convert_bitcast_fusion.2
  81.6 0.1 copy.52
  81.7 0.0 copy-done.6
  81.7 0.5 convert_bitcast_fusion.1
  82.2 0.1 copy.53
  82.3 1.1 reduce_sum.75
  83.4 0.0 copy-done
  83.4 0.6 convert_bitcast_fusion
  84.1 16.0 %all-to-all-done.1 = f32[16,32,768]{2,1,0:T(8,128)S(1)} async-done(((f32[16,32,768]{2,1,0:T(8,128)}), f32[16,32,768]{2,1,0:T(8,128)S(1)}, u32[]{:S(2)}, u32[]{:S(2)}) %all-to-all-start.1) | async-done | bytes 1572896 | tf_op jit(solution)/shard_map/all_to_all | solution.py:26
  100.1 0.1 reduce_sum.73
  100.2 0.0 copy-done.1
  100.2 0.0 copy-done.2
  100.2 0.0 copy-done.3
  100.2 0.6 fusion.3
  100.9 0.7 concatenate.17
  101.6 0.0 all-gather.2.cloned.1.call-update
  101.6 46.9 %all-gather.2.cloned.1.call-done = bf16[1024,1026]{1,0:T(8,128)(2,1)} async-done(((bf16[32,1026]{1,0:T(8,128)(2,1)}), bf16[1024,1026]{1,0:T(8,128)(2,1)}) %all-gather.2.cloned.1.call-update) | async-done | bytes 2101264 | tf_op jit(solution)/shard_map/all_gather | solution.py:41
  148.5 2.7 %slice_bitcast_fusion = (bf16[256,1024]{0,1:T(8,128)(2,1)S(1)}, bf16[1024,256]{1,0:T(8,128)(2,1)}, bf16[1024,256]{1,0:T(8,128)(2,1)}, bf16[1024,256]{1,0:T(8,128)(2,1)}) fusion(bf16[1024,1026]{1,0:T(8,128)(2,1)} %all-gather.2.cloned.1.call-done), kind=kLoop, calls=%fused_computation.1 | loop fusion | bytes 4194304 | tf_op jit(solution)/shard_map/transpose | solution.py:44
  151.2 1.0 copy.54
  152.2 1.9 %slice_reduce_fusion = (bf16[1024]{0:T(1024)(128)(2,1)}, bf16[1024]{0:T(1024)(128)(2,1)}) fusion(bf16[1024,1026]{1,0:T(8,128)(2,1)} %all-gather.2.cloned.1.call-done), kind=kLoop, calls=%fused_computation.2 | loop fusion | bytes 8192 | tf_op jit(solution)/shard_map/slice | solution.py:43
  (4 shorter events, 0.1 us)
Async XLA Ops:
  9.8 8.8 %all-to-all-start.4 = ((f32[2,1,512]{2,1,0:T(1,128)}), f32[2,1,512]{2,1,0:T(1,128)S(1)}, u32[]{:S(2)}, u32[]{:S(2)}) async-start(f32[2,1,512]{2,1,0:T(1,128)} %reshape.72), calls=%async_computation.4 | async-start | bytes 8192 | tf_op jit(solution)/shard_map/all_to_all | solution.py:19
  18.6 5.4 %copy-start.4 = (f32[1,1024]{1,0:T(1,128)S(1)}, f32[1,1024]{1,0:T(1,128)}, u32[]{:S(2)}) copy-start(f32[1,1024]{1,0:T(1,128)} %param.17) | copy-start | bytes 12292
  18.6 11.7 %all-to-all-start = ((f32[2,16,32,768]{3,2,1,0:T(8,128)}), f32[2,16,32,768]{3,2,1,0:T(8,128)S(1)}, u32[]{:S(2)}, u32[]{:S(2)}) async-start(f32[2,16,32,768]{3,2,1,0:T(8,128)} %copy.46), calls=%async_computation | async-start | bytes 6291456 | tf_op jit(solution)/shard_map/all_to_all | solution.py:19
  40.2 14.1 %all-to-all-start.5 = ((f32[16,1,32]{2,1,0:T(1,128)}), f32[16,1,32]{2,1,0:T(1,128)S(1)}, u32[]{:S(2)}, u32[]{:S(2)}) async-start(f32[16,1,32]{2,1,0:T(1,128)} %bitcast.10), calls=%async_computation.5 | async-start | bytes 16384 | tf_op jit(solution)/shard_map/all_to_all | solution.py:26
  54.3 9.8 %all-to-all-start.7 = ((f32[16,1,32]{2,1,0:T(1,128)}), f32[16,1,32]{2,1,0:T(1,128)S(1)}, u32[]{:S(2)}, u32[]{:S(2)}) async-start(f32[16,1,32]{2,1,0:T(1,128)} %bitcast.13), calls=%async_computation.7 | async-start | bytes 16384 | tf_op jit(solution)/shard_map/all_to_all | solution.py:26
  64.0 13.2 %all-to-all-start.3 = ((f32[16,256,32]{1,2,0:T(8,128)}), f32[16,256,32]{1,2,0:T(8,128)}, u32[]{:S(2)}, u32[]{:S(2)}) async-start(f32[16,256,32]{1,2,0:T(8,128)} %reduce_sum.74), calls=%async_computation.3 | async-start | bytes 1048576 | tf_op jit(solution)/shard_map/all_to_all | solution.py:26
  68.3 12.8 %copy-start.5 = (f32[32]{0:T(128)S(1)}, f32[32]{0:T(128)}, u32[]{:S(2)}) copy-start(f32[32]{0:T(128)} %param.22) | copy-start | bytes 388
  68.3 13.4 %copy-start.6 = (f32[32]{0:T(128)S(1)}, f32[32]{0:T(128)}, u32[]{:S(2)}) copy-start(f32[32]{0:T(128)} %param.23) | copy-start | bytes 388
  68.3 15.1 %copy-start = (f32[256,32]{0,1:T(8,128)S(1)}, f32[256,32]{0,1:T(8,128)}, u32[]{:S(2)}) copy-start(f32[256,32]{0,1:T(8,128)} %param.21) | copy-start | bytes 98308
  69.8 30.4 %copy-start.1 = (f32[32,256]{1,0:T(8,128)S(1)}, f32[32,256]{1,0:T(8,128)}, u32[]{:S(2)}) copy-start(f32[32,256]{1,0:T(8,128)} %param.20) | copy-start | bytes 98308
  69.8 30.4 %copy-start.2 = (f32[32,256]{1,0:T(8,128)S(1)}, f32[32,256]{1,0:T(8,128)}, u32[]{:S(2)}) copy-start(f32[32,256]{1,0:T(8,128)} %param.19) | copy-start | bytes 98308
  69.8 30.4 %copy-start.3 = (f32[32,256]{1,0:T(8,128)S(1)}, f32[32,256]{1,0:T(8,128)}, u32[]{:S(2)}) copy-start(f32[32,256]{1,0:T(8,128)} %param.18) | copy-start | bytes 98308
  77.3 22.8 %all-to-all-start.1 = ((f32[16,32,768]{2,1,0:T(8,128)}), f32[16,32,768]{2,1,0:T(8,128)S(1)}, u32[]{:S(2)}, u32[]{:S(2)}) async-start(f32[16,32,768]{2,1,0:T(8,128)} %reduce_sum.72), calls=%async_computation.1 | async-start | bytes 3145728 | tf_op jit(solution)/shard_map/all_to_all | solution.py:26
  81.0 67.5 %all-gather.2.cloned.1.call-start = ((), (), s32[]{:S(2)}) async-start(), calls=%async_computation.8 | async-start | bytes 2433024 | tf_op jit(solution)/shard_map/all_gather | solution.py:41
Sparse Core Ops, SparseCore 0:
  101.7 46.7 all-gather.1
where the time goes:
time: 162 us; the launch traced here: 161 us
  waiting for transfers between devices  79.5 us (49%)
  starting transfers between devices  27.8 us (17%)
  local copies, waits for them, and re-layouts  15.6 us (10%)
  between operations  14.2 us (9%)
  other arithmetic  13.9 us (9%)
  blocking collectives  9.91 us (6%)
    all_gather x1, waiting for transfers between devices, gather_turned(): whole, at, done = (lax.all_gather(both, axis, axis=0, tiled=True), 0, [])  46.9 us
    all_to_all x4, waiting for transfers between devices, sum_by_axis(): return jnp.sum(lax.all_to_all(own, far, 0, 0, tiled=True), axis=0)  32.6 us
    all_to_all x4, starting transfers between devices, sum_by_axis(): return jnp.sum(lax.all_to_all(own, far, 0, 0, tiled=True), axis=0)  19.1 us
    all_to_all x2, blocking collectives, sent_and_summed(): tiles = lax.all_to_all(in_blocks(x, dim, count), axis, 0, 0, tiled=True)  9.91 us
    all_to_all x2, starting transfers between devices, sent_and_summed(): tiles = lax.all_to_all(in_blocks(x, dim, count), axis, 0, 0, tiled=True)  8.68 us
    unnamed x21, local copies, waits for them, and re-layouts  5 us
    reduce_sum x4, other arithmetic, sent_and_summed(): return jnp.sum(tiles, axis=0)  4.88 us
    transpose x4, local copies, waits for them, and re-layouts, in_blocks(): return jnp.moveaxis(tiles, dim, 0)  4.34 us
  transfers between devices with their start and end apart: 7, of which 5 were waited for; matrix products, arithmetic and copies ran while one was open for 12% of the time, Pallas kernels for 0%

commit v1 on v0

--- a/solution.py
+++ b/solution.py
@@ -38,7 +38,13 @@
 def gather_turned(arrays, axis, dims):
     turned = [jnp.moveaxis(a, dim, 0) for a, dim in zip(arrays, dims)]
     both = jnp.concatenate([t.reshape(len(t), -1) for t in turned], axis=1)
-    whole, at, done = (lax.all_gather(both, axis, axis=0, tiled=True), 0, [])
+    whole, at, done = (
+        jnp.concatenate(
+            lax.all_to_all(jnp.stack([both] * lax.axis_size(axis)), axis, 0, 0), axis=0
+        ),
+        0,
+        [],
+    )
     for t, dim in zip(turned, dims):
         share = whole[:, at : at + t[0].size].reshape(-1, *t.shape[1:])
         done.append(jnp.moveaxis(share, 0, dim))

time: 162 us -> 138 us (0.85)
  waiting for transfers between devices: 79.5 us -> 32.7 us
  blocking collectives: 9.91 us -> 49.8 us
  between operations: 14.2 us -> 0.8 us
  local copies, waits for them, and re-layouts: 15.6 us -> 12.5 us
    all_gather x1 -> x0, waiting for transfers between devices: 46.9 us -> none  [gather_turned(): whole, at, done = (lax.all_gather(both, axis, axis=0, tiled=True), 0, [])]
    all_to_all x0 -> x1, blocking collectives: none -> 39.9 us  [gather_turned(): lax.all_to_all(jnp.stack([both] * lax.axis_size(axis)), axis, 0, 0)]
  transfers between devices with their start and end apart: 7 -> 6, of which waited for: 5 -> 4; matrix products, arithmetic and copies ran while one was open for 12% -> 14% of each run, Pallas kernels for 0% -> 0%
where the time goes in v1:
time: 138 us
  blocking collectives  49.8 us (36%)
  waiting for transfers between devices  32.7 us (24%)
  starting transfers between devices  27.8 us (20%)
  other arithmetic  13.9 us (10%)
  local copies, waits for them, and re-layouts  12.5 us (9%)
    all_to_all x1, blocking collectives, gather_turned(): lax.all_to_all(jnp.stack([both] * lax.axis_size(axis)), axis, 0, 0)  39.9 us
    all_to_all x4, waiting for transfers between devices, sum_by_axis(): return jnp.sum(lax.all_to_all(own, far, 0, 0, tiled=True), axis=0)  32.7 us
    all_to_all x4, starting transfers between devices, sum_by_axis(): return jnp.sum(lax.all_to_all(own, far, 0, 0, tiled=True), axis=0)  19.1 us
    all_to_all x2, blocking collectives, sent_and_summed(): tiles = lax.all_to_all(in_blocks(x, dim, count), axis, 0, 0, tiled=True)  9.91 us
    all_to_all x2, starting transfers between devices, sent_and_summed(): tiles = lax.all_to_all(in_blocks(x, dim, count), axis, 0, 0, tiled=True)  8.68 us
    unnamed x21, local copies, waits for them, and re-layouts  5 us
    reduce_sum x4, other arithmetic, sent_and_summed(): return jnp.sum(tiles, axis=0)  4.88 us
    transpose x4, local copies, waits for them, and re-layouts, in_blocks(): return jnp.moveaxis(tiles, dim, 0)  4.34 us
  transfers between devices with their start and end apart: 6, of which 4 were waited for; matrix products, arithmetic and copies ran while one was open for 14% of the time, Pallas kernels for 0%

profile of v1, /device:TPU:1, one launch (start us, length us, event | category | flops | bytes accessed | tf_op | source)
XLA Modules:
  0.0 137.6 jit_solution(982677774579907856)
XLA Ops:
  0.6 0.5 broadcast.20
  1.2 1.3 reduce.12
  2.5 0.1 reshape_reshape_squeeze.6
  2.6 0.7 reshape.78
  3.3 4.6 %all-to-all-start.4 = ((f32[2,1,512]{2,1,0:T(1,128)}), f32[2,1,512]{2,1,0:T(1,128)S(1)}, u32[]{:S(2)}, u32[]{:S(2)}) async-start(f32[2,1,512]{2,1,0:T(1,128)} %reshape.78), calls=%async_computation.4 | async-start | bytes 8192 | tf_op jit(solution)/shard_map/all_to_all | solution.py:19
  7.9 2.2 %maximum_bitcast_fusion = f32[2,16,32,768]{3,2,0,1:T(8,128)S(1)} fusion(f32[16,2,32,256]{3,2,1,0:T(8,128)} %bitcast.28, f32[16,2,32,256]{3,2,1,0:T(8,128)} %bitcast.29, f32[16,2,32,256]{3,2,1,0:T(8,128)} %bitcast.30), kind=kLoop, calls=%fused_computation | loop fusion | flops 1572864 | bytes 6291456 | tf_op jit(solution)/shard_map/transpose | solution.py:14
  10.1 2.0 %copy.53 = f32[2,16,32,768]{3,2,1,0:T(8,128)} copy(f32[2,16,32,768]{3,2,0,1:T(8,128)S(1)} %maximum_bitcast_fusion) | data formatting | bytes 6291456 | tf_op jit(solution)/shard_map/transpose | solution.py:14
  12.1 0.0 copy-start.4
  12.1 0.0 all-to-all-done.4
  12.1 4.1 %all-to-all-start = ((f32[2,16,32,768]{3,2,1,0:T(8,128)}), f32[2,16,32,768]{3,2,1,0:T(8,128)S(1)}, u32[]{:S(2)}, u32[]{:S(2)}) async-start(f32[2,16,32,768]{3,2,1,0:T(8,128)} %copy.53), calls=%async_computation | async-start | bytes 6291456 | tf_op jit(solution)/shard_map/all_to_all | solution.py:19
  16.2 0.5 broadcast.22
  16.7 0.7 reduce.14
  17.3 0.1 reshape.79
  17.4 0.0 copy-done.4
  17.4 0.7 reduce.13
  18.1 0.1 reshape_reshape_squeeze.7
  18.2 0.1 reshape.80
  18.3 2.5 %copy.54 = f32[1,256,1024]{1,2,0:T(8,128)} copy(f32[1,256,1024]{2,1,0:T(8,128)} %param.15) | data formatting | bytes 2097152 | tf_op args[3]
  20.8 2.3 %copy.55 = f32[2,16,256,32]{2,3,1,0:T(8,128)} copy(f32[2,16,256,32]{2,3,0,1:T(8,128)} %bitcast.27) | data formatting | bytes 2097152 | tf_op jit(solution)/shard_map/transpose | solution.py:14
  23.1 0.6 reduce_sum.76
  23.7 0.0 all-to-all-done
  23.7 3.4 %all_to_all.53 = f32[2,1,512]{2,1,0:T(1,128)S(1)} all-to-all(f32[2,1,512]{2,1,0:T(1,128)S(1)} %reshape.80), channel_id=1, replica_groups=mesh['batch_0'=4,'batch_1'=4,'batch_2'=2,'cols'=4] {'batch_2'}, dimensions={0} | all-to-all | bytes 8192 | tf_op jit(solution)/shard_map/all_to_all | solution.py:19
  27.1 6.5 %all_to_all.54 = f32[2,16,256,32]{2,3,1,0:T(8,128)} all-to-all(f32[2,16,256,32]{2,3,1,0:T(8,128)} %copy.55), channel_id=1, replica_groups=mesh['batch_0'=4,'batch_1'=4,'batch_2'=2,'cols'=4] {'batch_2'}, dimensions={0} | all-to-all | bytes 2097152 | tf_op jit(solution)/shard_map/all_to_all | solution.py:19
  33.6 7.7 %all-to-all-start.5 = ((f32[16,1,32]{2,1,0:T(1,128)}), f32[16,1,32]{2,1,0:T(1,128)S(1)}, u32[]{:S(2)}, u32[]{:S(2)}) async-start(f32[16,1,32]{2,1,0:T(1,128)} %bitcast.10), calls=%async_computation.5 | async-start | bytes 16384 | tf_op jit(solution)/shard_map/all_to_all | solution.py:26
  41.4 0.7 reduce.15
  42.0 0.1 reshape.81
  42.1 0.6 reduce_sum.78
  42.7 5.0 %all-to-all-done.5 = f32[16,1,32]{2,1,0:T(1,128)S(1)} async-done(((f32[16,1,32]{2,1,0:T(1,128)}), f32[16,1,32]{2,1,0:T(1,128)S(1)}, u32[]{:S(2)}, u32[]{:S(2)}) %all-to-all-start.5) | async-done | bytes 2080 | tf_op jit(solution)/shard_map/all_to_all | solution.py:26
  47.7 3.5 %all-to-all-start.7 = ((f32[16,1,32]{2,1,0:T(1,128)}), f32[16,1,32]{2,1,0:T(1,128)S(1)}, u32[]{:S(2)}, u32[]{:S(2)}) async-start(f32[16,1,32]{2,1,0:T(1,128)} %bitcast.13), calls=%async_computation.7 | async-start | bytes 16384 | tf_op jit(solution)/shard_map/all_to_all | solution.py:26
  51.2 2.1 %reduce_sum.74 = f32[16,256,32]{1,2,0:T(8,128)} reduce(f32[2,16,256,32]{2,3,1,0:T(8,128)} %all_to_all.54, f32[]{:T(128)} %constant.6.clone.1), dimensions={0}, to_apply=%region_2.0 | reduce | flops 131072 | bytes 1572868 | tf_op jit(solution)/shard_map/reduce_sum | solution.py:20
  53.3 4.2 %all-to-all-done.7 = f32[16,1,32]{2,1,0:T(1,128)S(1)} async-done(((f32[16,1,32]{2,1,0:T(1,128)}), f32[16,1,32]{2,1,0:T(1,128)S(1)}, u32[]{:S(2)}, u32[]{:S(2)}) %all-to-all-start.7) | async-done | bytes 2080 | tf_op jit(solution)/shard_map/all_to_all | solution.py:26
  57.5 4.2 %all-to-all-start.3 = ((f32[16,256,32]{1,2,0:T(8,128)}), f32[16,256,32]{1,2,0:T(8,128)}, u32[]{:S(2)}, u32[]{:S(2)}) async-start(f32[16,256,32]{1,2,0:T(8,128)} %reduce_sum.74), calls=%async_computation.3 | async-start | bytes 1048576 | tf_op jit(solution)/shard_map/all_to_all | solution.py:26
  61.7 0.0 copy-start.5
  61.8 0.0 copy-start.6
  61.8 0.0 copy-start
  61.8 1.5 %reduce_sum.72 = f32[16,32,768]{2,1,0:T(8,128)} reduce(f32[2,16,32,768]{3,2,1,0:T(8,128)S(1)} %all-to-all-done, f32[]{:T(128)} %constant.6.clone.1), dimensions={0}, to_apply=%region_0.0 | reduce | flops 393216 | bytes 4718596 | tf_op jit(solution)/shard_map/reduce_sum | solution.py:20
  63.3 0.0 copy-start.1
  63.3 0.0 copy-start.2
  63.3 0.0 copy-start.3
  63.3 7.4 %all-to-all-done.3 = f32[16,256,32]{1,2,0:T(8,128)} async-done(((f32[16,256,32]{1,2,0:T(8,128)}), f32[16,256,32]{1,2,0:T(8,128)}, u32[]{:S(2)}, u32[]{:S(2)}) %all-to-all-start.3) | async-done | bytes 524320 | tf_op jit(solution)/shard_map/all_to_all | solution.py:26
  70.7 3.7 %all-to-all-start.1 = ((f32[16,32,768]{2,1,0:T(8,128)}), f32[16,32,768]{2,1,0:T(8,128)S(1)}, u32[]{:S(2)}, u32[]{:S(2)}) async-start(f32[16,32,768]{2,1,0:T(8,128)} %reduce_sum.72), calls=%async_computation.1 | async-start | bytes 3145728 | tf_op jit(solution)/shard_map/all_to_all | solution.py:26
  74.5 0.0 copy-done.5
  74.5 0.5 convert_bitcast_fusion.2
  75.0 0.1 copy.59
  75.1 0.0 copy-done.6
  75.1 0.5 convert_bitcast_fusion.1
  75.7 0.1 copy.60
  75.8 1.1 reduce_sum.75
  76.8 0.0 copy-done
  76.9 0.6 convert_bitcast_fusion
  77.5 16.1 %all-to-all-done.1 = f32[16,32,768]{2,1,0:T(8,128)S(1)} async-done(((f32[16,32,768]{2,1,0:T(8,128)}), f32[16,32,768]{2,1,0:T(8,128)S(1)}, u32[]{:S(2)}, u32[]{:S(2)}) %all-to-all-start.1) | async-done | bytes 1572896 | tf_op jit(solution)/shard_map/all_to_all | solution.py:26
  93.6 0.1 reduce_sum.73
  93.7 0.0 copy-done.1
  93.7 0.0 copy-done.2
  93.7 0.0 copy-done.3
  93.7 0.6 fusion.3
  94.3 0.1 concatenate.17
  94.4 0.2 stack.2
  94.6 39.9 %all_to_all.55 = bf16[32,32,1026]{2,1,0:T(8,128)(2,1)S(1)} all-to-all(bf16[32,32,1026]{2,1,0:T(8,128)(2,1)S(1)} %stack.2), channel_id=1, replica_groups=mesh['batch_0'=4,'batch_1'=4,'batch_2'=2,'cols'=4] {'batch_0','batch_1',..., dimensions={0} | all-to-all | bytes 4202496 | tf_op jit(solution)/shard_map/all_to_all | solution.py:43
  134.5 1.2 slice_bitcast_fusion
  135.7 0.9 slice_reduce_fusion
  136.6 1.0 copy.61
  (4 shorter events, 0.1 us)
Async XLA Ops:
  3.3 8.8 %all-to-all-start.4 = ((f32[2,1,512]{2,1,0:T(1,128)}), f32[2,1,512]{2,1,0:T(1,128)S(1)}, u32[]{:S(2)}, u32[]{:S(2)}) async-start(f32[2,1,512]{2,1,0:T(1,128)} %reshape.78), calls=%async_computation.4 | async-start | bytes 8192 | tf_op jit(solution)/shard_map/all_to_all | solution.py:19
  12.1 5.4 %copy-start.4 = (f32[1,1024]{1,0:T(1,128)S(1)}, f32[1,1024]{1,0:T(1,128)}, u32[]{:S(2)}) copy-start(f32[1,1024]{1,0:T(1,128)} %param.17) | copy-start | bytes 12292
  12.1 11.7 %all-to-all-start = ((f32[2,16,32,768]{3,2,1,0:T(8,128)}), f32[2,16,32,768]{3,2,1,0:T(8,128)S(1)}, u32[]{:S(2)}, u32[]{:S(2)}) async-start(f32[2,16,32,768]{3,2,1,0:T(8,128)} %copy.53), calls=%async_computation | async-start | bytes 6291456 | tf_op jit(solution)/shard_map/all_to_all | solution.py:19
  33.6 14.1 %all-to-all-start.5 = ((f32[16,1,32]{2,1,0:T(1,128)}), f32[16,1,32]{2,1,0:T(1,128)S(1)}, u32[]{:S(2)}, u32[]{:S(2)}) async-start(f32[16,1,32]{2,1,0:T(1,128)} %bitcast.10), calls=%async_computation.5 | async-start | bytes 16384 | tf_op jit(solution)/shard_map/all_to_all | solution.py:26
  47.7 9.8 %all-to-all-start.7 = ((f32[16,1,32]{2,1,0:T(1,128)}), f32[16,1,32]{2,1,0:T(1,128)S(1)}, u32[]{:S(2)}, u32[]{:S(2)}) async-start(f32[16,1,32]{2,1,0:T(1,128)} %bitcast.13), calls=%async_computation.7 | async-start | bytes 16384 | tf_op jit(solution)/shard_map/all_to_all | solution.py:26
  57.5 13.2 %all-to-all-start.3 = ((f32[16,256,32]{1,2,0:T(8,128)}), f32[16,256,32]{1,2,0:T(8,128)}, u32[]{:S(2)}, u32[]{:S(2)}) async-start(f32[16,256,32]{1,2,0:T(8,128)} %reduce_sum.74), calls=%async_computation.3 | async-start | bytes 1048576 | tf_op jit(solution)/shard_map/all_to_all | solution.py:26
  61.7 12.8 %copy-start.5 = (f32[32]{0:T(128)S(1)}, f32[32]{0:T(128)}, u32[]{:S(2)}) copy-start(f32[32]{0:T(128)} %param.22) | copy-start | bytes 388
  61.8 13.4 %copy-start.6 = (f32[32]{0:T(128)S(1)}, f32[32]{0:T(128)}, u32[]{:S(2)}) copy-start(f32[32]{0:T(128)} %param.23) | copy-start | bytes 388
  61.8 15.1 %copy-start = (f32[256,32]{0,1:T(8,128)S(1)}, f32[256,32]{0,1:T(8,128)}, u32[]{:S(2)}) copy-start(f32[256,32]{0,1:T(8,128)} %param.21) | copy-start | bytes 98308
  63.3 30.4 %copy-start.1 = (f32[32,256]{1,0:T(8,128)S(1)}, f32[32,256]{1,0:T(8,128)}, u32[]{:S(2)}) copy-start(f32[32,256]{1,0:T(8,128)} %param.20) | copy-start | bytes 98308
  63.3 30.4 %copy-start.2 = (f32[32,256]{1,0:T(8,128)S(1)}, f32[32,256]{1,0:T(8,128)}, u32[]{:S(2)}) copy-start(f32[32,256]{1,0:T(8,128)} %param.19) | copy-start | bytes 98308
  63.3 30.4 %copy-start.3 = (f32[32,256]{1,0:T(8,128)S(1)}, f32[32,256]{1,0:T(8,128)}, u32[]{:S(2)}) copy-start(f32[32,256]{1,0:T(8,128)} %param.18) | copy-start | bytes 98308
  70.7 22.8 %all-to-all-start.1 = ((f32[16,32,768]{2,1,0:T(8,128)}), f32[16,32,768]{2,1,0:T(8,128)S(1)}, u32[]{:S(2)}, u32[]{:S(2)}) async-start(f32[16,32,768]{2,1,0:T(8,128)} %reduce_sum.72), calls=%async_computation.1 | async-start | bytes 3145728 | tf_op jit(solution)/shard_map/all_to_all | solution.py:26
